TPU v7x, 32 devices: a 4x4x1 block of a 4x4x8 slice. The times are simulated.
32 devices in a mesh: dp: 1 (over z), cp: 32 (over y, x, core).
Axes of the slice: x: 4, y: 4, z: 1, core: 2. Of those that a mesh axis runs over, the one named last changes fastest.
The devices are a block of a 4x4x8 slice.
Arguments:
- x: bfloat16 [8192, 3072], P(('dp', 'cp'))
- seg: int32 [8192], P(('dp', 'cp'))
- wq: bfloat16 [3072, 3072], replicated
- wk: bfloat16 [3072, 1024], replicated
- wv: bfloat16 [3072, 1024], replicated
- wo: bfloat16 [3072, 3072], replicated
Outputs:
- output: bfloat16 [8192, 3072], P(('dp', 'cp'))
All inputs are finite; a program needn't handle non-finite values.
Results may differ from a plain program's by a relative error of at most 0.00598599.
Values are sent between devices in bfloat16 or wider.
A program may use at most 768 MiB of HBM per device.

v0:
```python
import functools
import math

import jax
import jax.numpy as jnp
from jax import lax
from jax.experimental import pallas as pl
from jax.experimental.pallas import tpu as pltpu
from jax.sharding import PartitionSpec as P

DH = 128
PC = 128
KB = 4
MESH = pl.DeviceIdType.MESH
NEG_INF = float("-inf")
FLOOR = -3e38


class Place:
    def __init__(self, n):
        me = lax.axis_index("cp")
        self.n, self.side = n, math.isqrt(n // 2)
        self.me = me
        self.c = lax.rem(me, 2)
        chip = me // 2
        self.x = lax.rem(chip, self.side)
        self.y = chip // self.side
        self.xin = self.x + 1 - 2 * lax.rem(self.x, 2)
        self.xcross = self.side - 1 - self.x
        self.px = lax.rem(lax.rem(self.x, 2) + self.x // 2, 2)

    def dev(self, x, y, c):
        return (y * self.side + x) * 2 + c

    def row(self, dy):
        return lax.rem(self.y + dy + self.side, self.side)

    def col(self, dx):
        return self.xin if dx else self.x

    def peer(self, dx, dy):
        return self.dev(self.col(dx), self.row(dy), self.c)

    def head(self, dx, dy):
        return lax.rem(self.px + dx, 2) * self.side + self.row(dy)

    def slot(self, dx, dy):
        return self.row(dy) * 2 + lax.rem(self.x + dx, 2)


FAR = 2
KV_ORDER = (FAR, 0, 1, -1)
Q_ORDER = (FAR, 1, -1, 0)
O_ORDER = (1, -1, FAR, 0)


def _project(n, g, x_in, seg_ref, wk, wv, wq, kv_o, q_o, segs_o, x_ref, wkvb, wqb, kvacc, qacc, kvb, qb, skv, sq, rkv, rq, segb,
             x_sem, wkv_sem, wq_sem, kv_send, kv_recv, kvf_recv, rkv_recv, rkv_send, fx_send, fs_send,
             q_send, q_recv, qf_recv, rq_recv, rq_send, seg_send, seg_recv, out_sem, qout_sem):
    pt = Place(n)
    me = pt.me
    kv_steps = [(t, dx, dy) for t, dy in enumerate(KV_ORDER) for dx in range(2)]
    q_steps = [(t, dx, dy) for t, dy in enumerate(Q_ORDER) for dx in range(2)]
    own_kv = (KV_ORDER.index(0), 0)
    own_q = (Q_ORDER.index(0), 0)
    gd = g * DH
    kr = wqb.shape[1]
    nk = wqb.shape[0]
    my_head, my_slot = pt.head(0, 0), pt.slot(0, 0)

    kv_copies = [[pltpu.make_async_copy(w.at[pl.ds(t * kr, kr)], wkvb.at[i, t], wkv_sem.at[i, t]) for i, w in enumerate((wk, wv))]
                 for t in range(nk)]
    q_copies = [pltpu.make_async_copy(wq.at[pl.ds(t * kr, kr)], wqb.at[t], wq_sem.at[t]) for t in range(nk)]
    x_copy = pltpu.make_async_copy(x_in, x_ref, x_sem)
    x_copy.start()
    for cps in kv_copies:
        for cp in cps:
            cp.start()
    for cp in q_copies:
        cp.start()

    barrier = pltpu.get_barrier_semaphore()

    @pl.loop(1, n)
    def _(i):
        pl.semaphore_signal(barrier, inc=1, device_id={"cp": lax.rem(me + i, n)}, device_id_type=MESH)

    def seg_copy(i):
        return pltpu.make_async_remote_copy(seg_ref, segb.at[pl.ds(me, 1)], seg_send.at[i], seg_recv.at[me],
                                            device_id={"cp": lax.rem(me + i, n)}, device_id_type=MESH)

    segb[pl.ds(me, 1)] = seg_ref[...]

    def put(src, dst, send, recv, dev):
        return pltpu.make_async_remote_copy(src, dst, send, recv, device_id={"cp": dev}, device_id_type=MESH)

    def kv_copy(t, dx, dy):
        return put(skv.at[pt.head(dx, dy)], kvb.at[me], kv_send.at[2 * t + dx], kv_recv.at[me], pt.peer(dx, dy))

    def q_copy(t, dx, dy):
        return put(sq.at[pt.head(dx, dy)], qb.at[my_slot], q_send.at[2 * t + dx], q_recv.at[my_slot], pt.peer(dx, dy))

    way = (1, -1)
    hops = [(half, dx) for half in range(2) for dx in range(2)]

    def kv_hop(half, dx):
        return put(skv.at[pt.head(dx, FAR), half], rkv.at[half, dx], kv_send.at[2 * half + dx if half == 0 else 2 * len(KV_ORDER) + dx],
                   rkv_recv.at[half, dx], pt.peer(0, way[half]))

    def kv_hand(half, dx):
        return put(rkv.at[half, dx], kvb.at[pt.peer(0, -way[half]), half], rkv_send.at[half, dx], kvf_recv.at[dx, half],
                   pt.peer(dx, way[half]))

    def q_hop(half, dx):
        return put(sq.at[pt.head(dx, FAR), half], rq.at[half, dx], q_send.at[2 * half + dx if half == 0 else 2 * len(Q_ORDER) + dx],
                   rq_recv.at[half, dx], pt.peer(0, way[half]))

    def q_hand(half, dx):
        return put(rq.at[half, dx], qb.at[pt.slot(0, -way[half]), half], rq_send.at[half, dx], qf_recv.at[dx, half],
                   pt.peer(dx, way[half]))

    nb = 4 * DH

    def summed(t, w, acc, c):
        cols = slice(c * nb, (c + 1) * nb)
        r = jnp.dot(x_ref[:, t * kr:(t + 1) * kr], w[:, cols], preferred_element_type=jnp.float32)
        if t > 0:
            r = r + acc[:, cols]
        if t < nk - 1:
            acc[:, cols] = r
        return r

    def kv_step(t):
        for cp in kv_copies[t]:
            cp.wait()
        for c in range(wkvb.shape[3] // nb):
            for i in range(2):
                r = summed(t, wkvb.at[i, t], kvacc.at[i], c)
                if t == nk - 1:
                    for u in range(nb // DH):
                        part = r[:, u * DH:(u + 1) * DH]
                        part = (jnp.transpose(part) if i == 1 else part).astype(jnp.bfloat16)
                        for half in range(2):
                            rows = slice(half * PC, (half + 1) * PC)
                            skv[c * (nb // DH) + u, half, i] = part[:, rows] if i == 1 else part[rows]

    def q_step(t, first, last):
        if first == 0:
            q_copies[t].wait()
        for c in range(first, last):
            r = summed(t, wqb.at[t], qacc, c)
            if t == nk - 1:
                for u in range(nb // DH):
                    col = c * (nb // DH) + u
                    part = jnp.transpose(r[:, u * DH:(u + 1) * DH]).astype(jnp.bfloat16)
                    for half in range(2):
                        sq[col // g, half, col % g] = part[:, half * PC:(half + 1) * PC]

    def send_kv(t):
        if KV_ORDER[t] == FAR:
            for hop in hops:
                kv_hop(*hop).start()
        else:
            for dx in range(2):
                if (t, dx) != own_kv:
                    kv_copy(t, dx, KV_ORDER[t]).start()

    def send_q(t):
        if Q_ORDER[t] == FAR:
            for hop in hops:
                q_hop(*hop).start()
        else:
            for dx in range(2):
                if (t, dx) != own_q:
                    q_copy(t, dx, Q_ORDER[t]).start()

    def to_cross(src, i):
        return put(kvb.at[src], kvb.at[src], fx_send.at[i], kv_recv.at[src], pt.dev(pt.xcross, pt.y, pt.c))

    def to_sibling(src, i):
        return put(kvb.at[src], kvb.at[src], fs_send.at[i], kv_recv.at[src], pt.dev(pt.x, pt.y, 1 - pt.c))

    def kv_out(src):
        return pltpu.make_async_copy(kvb.at[src], kv_o.at[src], out_sem.at[src])

    def q_out(slot):
        return pltpu.make_async_copy(qb.at[slot], q_o.at[slot], qout_sem.at[slot])

    def arrived(src):
        to_sibling(src, 0).wait_recv()

    def forward(t):
        dy = KV_ORDER[t]
        for dx in range(2):
            src = pt.peer(dx, -dy)
            if dy == FAR:
                for half in range(2):
                    put(rkv.at[half, dx], kvb.at[src, half], rkv_send.at[half, dx], kvf_recv.at[dx, half], me).wait_recv()
            elif (t, dx) != own_kv:
                arrived(src)
            to_cross(src, 2 * t + dx).start()
            to_sibling(src, 2 * t + dx).start()
            kv_out(src).start()

    def own_out():
        return pltpu.make_async_copy(skv.at[my_head], kv_o.at[me], out_sem.at[me])

    def own_q_out():
        return pltpu.make_async_copy(sq.at[my_head], q_o.at[my_slot], qout_sem.at[my_slot])

    def forward_own():
        put(skv.at[my_head], kvb.at[me], fx_send.at[2 * own_kv[0]], kv_recv.at[me], pt.dev(pt.xcross, pt.y, pt.c)).start()
        put(skv.at[my_head], kvb.at[me], fs_send.at[2 * own_kv[0]], kv_recv.at[me], pt.dev(pt.x, pt.y, 1 - pt.c)).start()
        own_out().start()

    def forward_next():
        src = pt.peer(1, 0)
        arrived(src)
        to_cross(src, 2 * own_kv[0] + 1).start()
        to_sibling(src, 2 * own_kv[0] + 1).start()
        kv_out(src).start()

    x_copy.wait()
    for t in range(nk):
        kv_step(t)
    nq = wqb.shape[2] // nb

    pl.semaphore_wait(barrier, n - 1)
    for t in range(len(KV_ORDER)):
        send_kv(t)
    forward_own()
    q_step(0, 0, nq)
    q_step(1, 0, nq)
    q_step(2, 0, nq)
    forward_next()
    for hop in hops:
        put(rkv.at[hop], rkv.at[hop], kv_send.at[0], rkv_recv.at[hop], me).wait_recv()
        kv_hand(*hop).start()
    q_step(3, 0, nq)
    own_q_out().start()
    forward(2)
    forward(3)
    forward(0)
    send_q(0)
    send_q(1)

    def mirrored(dx, dy, c):
        x = pt.side - 1 - pt.col(dx)
        return pt.dev(x, pt.row(-dy), c)

    passing = [(t, dx, KV_ORDER[t]) for t in (1, 2, 3, 0) for dx in range(2)]

    def pass_on(steps):
        for t, dx, dy in steps:
            src = mirrored(dx, dy, pt.c)
            arrived(src)
            to_sibling(src, 8 + 2 * t + dx).start()
            kv_out(src).start()

    pass_on(passing[:4])
    send_q(2)
    for hop in hops:
        put(rq.at[hop], rq.at[hop], q_send.at[0], rq_recv.at[hop], me).wait_recv()
        q_hand(*hop).start()
    send_q(3)
    pass_on(passing[4:])

    @pl.loop(1, n)
    def _(i):
        seg_copy(i).start()

    for t, dx, dy in passing:
        src = pt.dev(pt.col(dx), pt.row(-dy), 1 - pt.c)
        arrived(src)
        kv_out(src).start()
    for t, dx, dy in q_steps:
        slot = pt.slot(dx, -dy)
        if dy == FAR:
            for half in range(2):
                put(rq.at[half, dx], qb.at[slot, half], rq_send.at[half, dx], qf_recv.at[dx, half], me).wait_recv()
        elif (t, dx) != own_q:
            put(qb.at[slot], qb.at[slot], q_send.at[0], q_recv.at[slot], me).wait_recv()
        if (t, dx) != own_q:
            q_out(slot).start()
    for t, dx, dy in passing:
        src = mirrored(dx, dy, 1 - pt.c)
        arrived(src)
        kv_out(src).start()

    @pl.loop(1, n)
    def _(i):
        src = lax.rem(me + i, n)
        pltpu.make_async_remote_copy(seg_ref, segb.at[pl.ds(src, 1)], seg_send.at[i], seg_recv.at[src],
                                     device_id={"cp": src}, device_id_type=MESH).wait_recv()

    segs_o[...] = segb[...]

    @pl.loop(1, n)
    def _(i):
        seg_copy(i).wait_send()

    for hop in hops:
        kv_hop(*hop).wait_send()
        kv_hand(*hop).wait_send()
        q_hop(*hop).wait_send()
        q_hand(*hop).wait_send()
    for t, dx, dy in kv_steps:
        if dy != FAR and (t, dx) != own_kv:
            kv_copy(t, dx, dy).wait_send()
        src = pt.peer(dx, -dy)
        to_cross(src, 2 * t + dx).wait_send()
        to_sibling(src, 2 * t + dx).wait_send()
        to_sibling(src, 8 + 2 * t + dx).wait_send()
    for t, dx, dy in q_steps:
        if dy != FAR and (t, dx) != own_q:
            q_copy(t, dx, dy).wait_send()

    @pl.loop(0, n)
    def _(i):
        kv_out(i).wait()

    @pl.loop(0, n // 4)
    def _(i):
        q_out(i).wait()


class Pairs:
    def __init__(self, pt, n, g, scale, first_of, seg_v, kvs, qs, t_sc, acc_sc):
        self.pt, self.n, self.g, self.scale, self.first_of, self.seg_v, self.kvs = pt, n, g, scale, first_of, seg_v, kvs
        self.qs, self.t_sc, self.acc_sc = qs, t_sc, acc_sc

    def begins(self, row, half):
        out = []
        for u in range(2):
            src = self.pt.dev((self.pt.x // 2) * 2 + u, row, self.pt.c)
            before = jnp.where(self.seg_v[...] < self.first_of(src, half), 1.0, 0.0)
            out.append(jnp.sum(before).astype(jnp.int32))
        return out

    def __call__(self, row, half, lo, begins, store):
        pt, n, g, scale, seg_v, kvs, qs = self.pt, self.n, self.g, self.scale, self.seg_v, self.kvs, self.qs
        t_sc, acc_sc = self.t_sc, self.acc_sc
        last_piece, pieces = 2 * n - 1, kvs.shape[0]
        srcs = [pt.dev((pt.x // 2) * 2 + u, row, pt.c) for u in range(2)]
        ps = [last_piece - src if half else src for src in srcs]
        end = jnp.maximum(ps[0], ps[1])
        wide = g * PC
        acc_sc[...] = jnp.zeros_like(acc_sc)

        def queries(us):
            return jnp.concatenate([qs[2 * row + u, w] for u in us for w in range(g)], axis=1)

        def start(b):
            return jnp.minimum(lo + b * KB, pieces - KB)

        def scores(b):
            j0, js = lo + b * KB, start(b)
            k = jnp.concatenate([kvs[js + w, 0] for w in range(KB)], axis=0)
            s = jnp.dot(k, queries((0, 1)), preferred_element_type=jnp.float32) * scale
            pos = lax.broadcasted_iota(jnp.int32, (KB * PC, DH), 0) + js * PC
            tops = []
            for u in range(2):
                seen = (pos >= jnp.maximum(begins[u], j0 * PC)) & (pos < ps[u] * PC)
                for w in range(g):
                    at = slice(u * wide + w * PC, u * wide + (w + 1) * PC)
                    part = jnp.where(seen, s[:, at], NEG_INF)
                    t_sc[:, at] = part
                    tops.append(jnp.max(part, axis=0, keepdims=True))
            return jnp.concatenate(tops, axis=1)

        def step(b, carry):
            m, l, top = carry
            js = start(b)
            m_new = jnp.maximum(m, top)
            corr = jnp.exp2(m - m_new)
            p = jnp.exp2(t_sc[...] - m_new)
            l = l * corr + jnp.sum(p, axis=0, keepdims=True)
            vt = jnp.concatenate([kvs[js + w, 1] for w in range(KB)], axis=1)
            acc_sc[...] = acc_sc[...] * corr + jnp.dot(vt, p.astype(jnp.bfloat16), preferred_element_type=jnp.float32)
            return m_new, l, scores(b + 1)

        line = jnp.zeros((1, 2 * wide), jnp.float32)
        m, l, _ = lax.fori_loop(0, lax.div(end - lo + KB - 1, KB), step, (line + FLOOR, line, scores(0)))

        key = lax.broadcasted_iota(jnp.int32, (PC, PC), 0)
        query = lax.broadcasted_iota(jnp.int32, (PC, PC), 1)
        ss = [jnp.dot(kvs[ps[u], 0], queries((u,)), preferred_element_type=jnp.float32) * scale for u in range(2)]
        for u in range(2):
            at = slice(u * wide, (u + 1) * wide)
            ids = seg_v[srcs[u], pl.ds(half, 1), :]
            idb = jnp.broadcast_to(ids, (PC, PC))
            allowed = jnp.concatenate([(idb == jnp.transpose(idb)) & (key <= query)] * g, axis=1)
            keep = jnp.concatenate([ids == self.first_of(srcs[u], half)] * g, axis=1)
            s = jnp.where(allowed, ss[u], NEG_INF)
            m_old = jnp.where(keep, m[:, at], FLOOR)
            m_new = jnp.maximum(m_old, jnp.max(s, axis=0, keepdims=True))
            corr = jnp.where(keep, jnp.exp2(m_old - m_new), 0.0)
            p = jnp.exp2(s - m_new)
            ll = l[:, at] * corr + jnp.sum(p, axis=0, keepdims=True)
            acc = acc_sc[:, at] * corr + jnp.dot(kvs[ps[u], 1], p.astype(jnp.bfloat16), preferred_element_type=jnp.float32)
            o = acc * (1.0 / ll)
            for w in range(g):
                store(u, w, jnp.transpose(o[:, w * PC:(w + 1) * PC]).astype(jnp.bfloat16))


def _pair_scratch(g):
    f32 = jnp.float32
    return [pltpu.VMEM((KB * PC, 2 * g * PC), f32), pltpu.VMEM((DH, 2 * g * PC), f32)]


def _attend(n, g, scale, segs, kv, q_in, o_out, seg_s, seg_v, kvs, qs, os, lo_s, t_sc, acc_sc,
            seg_sem, kv_sem, q_sem, o_sem):
    pt = Place(n)
    last_piece = 2 * n - 1
    ng = q_in.shape[0]

    def load(p):
        owner = jnp.where(p < n, p, last_piece - p)
        return pltpu.make_async_copy(kv.at[owner, jnp.where(p < n, 0, 1)], kvs.at[p], kv_sem)

    seg_copies = [pltpu.make_async_copy(segs, seg_v, seg_sem.at[0]), pltpu.make_async_copy(segs, seg_s, seg_sem.at[1])]
    q_copies = [pltpu.make_async_copy(q_in.at[i, 1], qs.at[i], q_sem) for i in range(ng)]
    for cp in seg_copies + q_copies:
        cp.start()

    @pl.loop(0, 2 * n)
    def _(p):
        load(p).start()

    for cp in seg_copies:
        cp.wait()
    pairs = Pairs(pt, n, g, scale, lambda src, half: seg_s[src, half, 0], seg_v, kvs, qs, t_sc, acc_sc)
    for i in range(ng // 2):
        for u, at in enumerate(pairs.begins(i, 1)):
            lo_s[2 * i + u] = at
    for cp in q_copies:
        cp.wait()

    @pl.loop(0, 2 * n)
    def _(p):
        load(p).wait()

    def out(slot):
        return pltpu.make_async_copy(os.at[slot], o_out.at[slot], o_sem)

    def one(row, carry):
        def store(u, w, val):
            os[2 * row + u, :, w * DH:(w + 1) * DH] = val

        begins = [lo_s[2 * row + u] for u in range(2)]
        pairs(row, 1, lax.div(jnp.minimum(*begins), PC), begins, store)

        @pl.when(row > 0)
        def _():
            for u in range(2):
                out(2 * (row - 1) + u).start()

        return carry

    lax.fori_loop(0, ng // 2, one, 0)
    for u in range(2):
        out(ng - 2 + u).start()
    for i in range(ng):
        out(i).wait()


def _combine(n, g, scale, segs, kv, q_in, o_in, wo, y_ref, obuf, robuf, ol, wob, acc, seg_s, seg_v, kvs, qs,
             t_sc, acc_sc, w_sem, o_send, o_recv, ro_recv, ro_send, seg_sem, kv_sem, q_sem):
    pt = Place(n)
    me = pt.me
    gd = g * DH
    ng = q_in.shape[0]
    my_head, my_slot = pt.head(0, 0), pt.slot(0, 0)
    nc = 4
    wn = y_ref.shape[1] // nc
    lows, highs = pl.ds(0, PC), pl.ds(PC, PC)

    def load(p):
        return pltpu.make_async_copy(kv.at[p, 0], kvs.at[p], kv_sem.at[p])

    q_copies = [pltpu.make_async_copy(q_in.at[i, 0], qs.at[i], q_sem.at[i]) for i in range(ng)]
    seg_copies = [pltpu.make_async_copy(segs, seg_v, seg_sem.at[0]), pltpu.make_async_copy(segs, seg_s, seg_sem.at[1])]
    own = pltpu.make_async_copy(o_in.at[my_slot], obuf.at[my_head, highs], o_recv.at[1, my_head])
    for cp in seg_copies + q_copies + [own]:
        cp.start()

    @pl.loop(0, n)
    def _(p):
        load(p).start()

    def w_copies(t):
        for dx in range(2):
            h = pl.multiple_of(pt.head(dx, O_ORDER[t]) * gd, gd)
            yield pltpu.make_async_copy(wo.at[pl.ds(h, gd), :], wob.at[t, pl.ds(dx * gd, gd), :], w_sem.at[t, dx])

    for t in range(len(O_ORDER)):
        for cp in w_copies(t):
            cp.start()

    others = [(dx, dy) for dy in O_ORDER for dx in range(2) if (dx, dy) != (0, 0)]
    near = [s for s in others if s[1] != FAR]
    barrier = pltpu.get_barrier_semaphore()
    for dx, dy in others:
        pl.semaphore_signal(barrier, inc=1, device_id={"cp": pt.peer(dx, dy)}, device_id_type=MESH)
    pl.semaphore_wait(barrier, len(others))

    def put(src, dst, send, recv, dev):
        return pltpu.make_async_remote_copy(src, dst, send, recv, device_id={"cp": dev}, device_id_type=MESH)

    way = (1, -1)
    turn = {FAR: 0, 1: 1, -1: 2, 0: 3}

    def source(half, dx, dy):
        return o_in.at[pt.slot(dx, dy)] if half else ol.at[turn[dy], lax.rem(pt.x + dx, 2)]

    def o_copy(half, i):
        dx, dy = near[i]
        return put(source(half, dx, dy), obuf.at[my_head, highs if half else lows], o_send.at[half, i], o_recv.at[half, my_head],
                   pt.peer(dx, dy))

    def o_hop(half, dx):
        return put(source(half, dx, FAR), robuf.at[half, dx], o_send.at[half, len(near) + dx], ro_recv.at[half, dx],
                   pt.peer(0, way[dx]))

    def o_hand(half, dx):
        head = pt.head(0, -way[dx])
        return put(robuf.at[half, dx], obuf.at[head, highs if half else lows], ro_send.at[half, dx], o_recv.at[half, head],
                   pt.peer(dx, way[dx]))

    def hand_on(half):
        for dx in range(2):
            put(robuf.at[half, dx], robuf.at[half, dx], o_send.at[0, 0], ro_recv.at[half, dx], me).wait_recv()
            o_hand(half, dx).start()

    for dx in range(2):
        o_hop(1, dx).start()
    for i in range(len(near)):
        o_copy(1, i).start()

    for cp in seg_copies + q_copies:
        cp.wait()

    @pl.loop(0, n)
    def _(p):
        load(p).wait()

    pairs = Pairs(pt, n, g, scale, lambda src, half: seg_s[src, half, 0], seg_v, kvs, qs, t_sc, acc_sc)

    def send_low(dy):
        if dy == FAR:
            for dx in range(2):
                o_hop(0, dx).start()
        else:
            for i, (dx, to) in enumerate(near):
                if to == dy:
                    o_copy(0, i).start()

    def one(i, carry):
        turned = jnp.where(i == 2, -1, jnp.where(i == 3, 0, FAR - i))
        row = lax.rem(pt.y + turned + pt.side, pt.side)

        def store(u, w, val):
            ol[i, u, :, w * DH:(w + 1) * DH] = val

        pairs(row, 0, 0, pairs.begins(row, 0), store)

        @pl.when(i == 1)
        def _():
            send_low(FAR)
            hand_on(1)

        @pl.when(i == 2)
        def _():
            send_low(1)

        @pl.when(i == 3)
        def _():
            send_low(-1)
            hand_on(0)

        return carry

    lax.fori_loop(0, ng // 2, one, 0)
    send_low(0)
    obuf[my_head, 0:PC] = ol[turn[0], lax.rem(pt.x, 2)]

    for t, dy in enumerate(O_ORDER):
        for cp in w_copies(t):
            cp.wait()
        heads = [pt.head(dx, dy) for dx in range(2)]
        for dx in range(2):
            if dy == 0 and dx == 0:
                own.wait()
            else:
                for half in range(2):
                    put(ol.at[0, 0], obuf.at[heads[dx], highs if half else lows], o_send.at[0, 0], o_recv.at[half, heads[dx]],
                        me).wait_recv()
        a = jnp.concatenate([obuf[heads[0]], obuf[heads[1]]], axis=1)
        for u in range(nc):
            r = jnp.dot(a, wob[t, :, u * wn:(u + 1) * wn], preferred_element_type=jnp.float32)
            if t > 0:
                r = r + acc[:, u * wn:(u + 1) * wn]
            if t < len(O_ORDER) - 1:
                acc[:, u * wn:(u + 1) * wn] = r
            else:
                y_ref[:, u * wn:(u + 1) * wn] = r.astype(y_ref.dtype)
    for half in range(2):
        for i in range(len(near)):
            o_copy(half, i).wait_send()
        for dx in range(2):
            o_hop(half, dx).wait_send()
            o_hand(half, dx).wait_send()


def solution(mesh):
    n = mesh.shape["cp"]
    side = math.isqrt(n // 2)
    bf, f32 = jnp.bfloat16, jnp.float32
    vmem, anym = pl.BlockSpec(memory_space=pltpu.VMEM), pl.BlockSpec(memory_space=pltpu.HBM)
    dma = pltpu.SemaphoreType.DMA

    def local(x, seg, wq, wk, wv, wo):
        lq, d = x.shape
        hkv = wk.shape[1] // DH
        g = wq.shape[1] // wk.shape[1]
        gd = g * DH
        ng = 2 * side
        kv, q, segs = pl.pallas_call(
            functools.partial(_project, n, g),
            out_shape=(jax.ShapeDtypeStruct((n, 2, 2, PC, DH), bf), jax.ShapeDtypeStruct((ng, 2, g, PC, DH), bf),
                       jax.ShapeDtypeStruct((n, 2, PC), jnp.int32)),
            in_specs=[anym, vmem, anym, anym, anym],
            out_specs=(anym, anym, vmem),
            scratch_shapes=[
                pltpu.VMEM((lq, d), bf),
                pltpu.VMEM((2, side, d // side, hkv * DH), bf), pltpu.VMEM((side, d // side, hkv * gd), bf),
                pltpu.VMEM((2, lq, hkv * DH), f32), pltpu.VMEM((lq, hkv * gd), f32),
                pltpu.VMEM((n, 2, 2, PC, DH), bf), pltpu.VMEM((ng, 2, g, PC, DH), bf),
                pltpu.VMEM((ng, 2, 2, PC, DH), bf), pltpu.VMEM((ng, 2, g, PC, DH), bf),
                pltpu.VMEM((2, 2, 2, PC, DH), bf), pltpu.VMEM((2, 2, g, PC, DH), bf), pltpu.VMEM((n, 2, PC), jnp.int32),
                dma, dma((2, side)), dma((side,)), dma((ng + 2,)), dma((n,)), dma((2, 2)), dma((2, 2)), dma((2, 2)),
                dma((ng,)), dma((2 * ng,)),
                dma((ng + 2,)), dma((ng,)), dma((2, 2)), dma((2, 2)), dma((2, 2)), dma((n,)), dma((n,)), dma((n,)), dma((ng,)),
            ],
            compiler_params=pltpu.CompilerParams(collective_id=0, has_side_effects=True, vmem_limit_bytes=60 << 20),
            name="project",
        )(x, seg.reshape(1, 2, PC), wk, wv, wq)
        scale = DH ** -0.5 * math.log2(math.e)
        o = pl.pallas_call(
            functools.partial(_attend, n, g, scale),
            out_shape=jax.ShapeDtypeStruct((ng, PC, gd), bf),
            in_specs=[anym] * 3,
            out_specs=anym,
            scratch_shapes=[pltpu.SMEM((n, 2, PC), jnp.int32), pltpu.VMEM((n, 2, PC), jnp.int32),
                            pltpu.VMEM((2 * n, 2, PC, DH), bf), pltpu.VMEM((ng, g, PC, DH), bf),
                            pltpu.VMEM((ng, PC, gd), bf), pltpu.SMEM((ng,), jnp.int32)] + _pair_scratch(g) + [dma((2,)), dma, dma, dma],
            compiler_params=pltpu.CompilerParams(vmem_limit_bytes=60 << 20),
            name="attend",
        )(segs, kv, q)
        return pl.pallas_call(
            functools.partial(_combine, n, g, scale),
            out_shape=jax.ShapeDtypeStruct((lq, wo.shape[1]), bf),
            in_specs=[anym] * 5,
            out_specs=vmem,
            scratch_shapes=[pltpu.VMEM((hkv, lq, gd), bf), pltpu.VMEM((2, 2, PC, gd), bf), pltpu.VMEM((ng // 2, 2, PC, gd), bf),
                            pltpu.VMEM((side, 2 * gd, wo.shape[1]), bf), pltpu.VMEM((lq, wo.shape[1]), f32),
                            pltpu.SMEM((n, 2, PC), jnp.int32), pltpu.VMEM((n, 2, PC), jnp.int32),
                            pltpu.VMEM((n, 2, PC, DH), bf), pltpu.VMEM((ng, g, PC, DH), bf)] + _pair_scratch(g) + [
                            dma((side, 2)), dma((2, ng)), dma((2, ng)), dma((2, 2)), dma((2, 2)), dma((2,)), dma((n,)), dma((ng,))],
            compiler_params=pltpu.CompilerParams(collective_id=1, has_side_effects=True, vmem_limit_bytes=60 << 20),
            name="combine",
        )(segs, kv, q, o, wo)

    rows = P(("dp", "cp"), None)
    return jax.shard_map(local, mesh=mesh, in_specs=(rows, P(("dp", "cp")), P(), P(), P(), P()), out_specs=rows, check_vma=False)
```

profile of v0, /device:TPU:100, one launch (start us, length us, event | category | flops | bytes accessed | tf_op | source)
XLA Modules:
  0.0 100.1 jit_solution(15797024025342016274)
XLA Ops:
  0.0 54.6 %project.1 = (bf16[32,2,2,128,128]{4,3,2,1,0:T(8,128)(2,1)}, bf16[8,2,3,128,128]{4,3,2,1,0:T(8,128)(2,1)}, s32[32,2,128]{2,1,0:T(2,128)}) custom-call(bf16[256,3072]{1,0:T(8,128)(2,1)} %x_in.1, s32[1,2,128]{2,1,0:T(2,128)} %bitcast.1, bf16[3072,1024]{1,0:T(8,128)(2,1)} %wk.1, bf16[3072,1024]{1,0:T(8,128)(2,1)} %wv.1, bf16[3072,3072]{1,0:T(8,128)(2,1)} %wq.1), custom_call_target="tpu_custom_call" | custom-call | tf_op jit(solution)/shard_map/project/pallas_call | solution.py:628
  54.6 9.6 %attend.1.o_in = bf16[8,128,384]{2,1,0:T(8,128)(2,1)} custom-call(s32[32,2,128]{2,1,0:T(2,128)} %get-tuple-element.8.segs, bf16[32,2,2,128,128]{4,3,2,1,0:T(8,128)(2,1)} %get-tuple-element.9.kv, bf16[8,2,3,128,128]{4,3,2,1,0:T(8,128)(2,1)} %get-tuple-element.10.q_in), custom_call_target="tpu_custom_call" | custom-call | tf_op jit(solution)/shard_map/attend/pallas_call | solution.py:649
  64.2 33.2 %combine.1 = bf16[256,3072]{1,0:T(8,128)(2,1)} custom-call(s32[32,2,128]{2,1,0:T(2,128)} %get-tuple-element.8.segs, bf16[32,2,2,128,128]{4,3,2,1,0:T(8,128)(2,1)} %get-tuple-element.9.kv, bf16[8,2,3,128,128]{4,3,2,1,0:T(8,128)(2,1)} %get-tuple-element.10.q_in, bf16[8,128,384]{2,1,0:T(8,128)(2,1)} %attend.1.o_in, bf16[3072,3072]{1,0:T(8,128)(2,1)} %wo.1), custom_call_target="tpu_custom_call" | custom-call | tf_op jit(solution)/shard_map/combine/pallas_call | solution.py:660
  97.4 2.7 %copy.8 = bf16[256,3072]{1,0:T(8,128)(2,1)} copy(bf16[256,3072]{1,0:T(8,128)(2,1)} %combine.1) | data formatting | bytes 3145728
where the time goes:
time: 100 us
  Pallas kernels  97.4 us (97%)
  local copies, waits for them, and re-layouts  2.65 us (3%)
    pallas_call x1, Pallas kernels, local(): pl.pallas_call(functools.partial(_project, n, g), out_shape=(jax.ShapeDty...  54.6 us
    pallas_call x1, Pallas kernels, local(): pl.pallas_call(functools.partial(_combine, n, g, scale), out_shape=jax.Sh...  33.2 us
    pallas_call x1, Pallas kernels, local(): pl.pallas_call(functools.partial(_attend, n, g, scale), out_shape=jax.Sha...  9.64 us
    unnamed x1, local copies, waits for them, and re-layouts  2.65 us

commit v1 on v0

--- a/solution.py
+++ b/solution.py
@@ -238,11 +238,13 @@
         kv_hand(*hop).start()
     q_step(3, 0, nq)
     own_q_out().start()
+    send_q(0)
     forward(2)
+    send_q(1)
     forward(3)
+    send_q(2)
     forward(0)
-    send_q(0)
-    send_q(1)
+    send_q(3)
 
     def mirrored(dx, dy, c):
         x = pt.side - 1 - pt.col(dx)
@@ -258,11 +260,9 @@
             kv_out(src).start()
 
     pass_on(passing[:4])
-    send_q(2)
     for hop in hops:
         put(rq.at[hop], rq.at[hop], q_send.at[0], rq_recv.at[hop], me).wait_recv()
         q_hand(*hop).start()
-    send_q(3)
     pass_on(passing[4:])
 
     @pl.loop(1, n)

time: 100 us -> 98.9 us (0.989)
  Pallas kernels: 97.4 us -> 96.1 us
    pallas_call x1, Pallas kernels: 54.6 us -> 52.3 us  [local(): pl.pallas_call(functools.partial(_project, n, g), out_shape=(jax.ShapeDty...]
    pallas_call x1, Pallas kernels: 33.2 us -> 34.2 us  [local(): pl.pallas_call(functools.partial(_combine, n, g, scale), out_shape=jax.Sh...]
where the time goes in v1:
time: 98.9 us; the launch traced here: 98.8 us
  Pallas kernels  96.1 us (97%)
  local copies, waits for them, and re-layouts  2.65 us (3%)
    pallas_call x1, Pallas kernels, local(): pl.pallas_call(functools.partial(_project, n, g), out_shape=(jax.ShapeDty...  52.3 us
    pallas_call x1, Pallas kernels, local(): pl.pallas_call(functools.partial(_combine, n, g, scale), out_shape=jax.Sh...  34.2 us
    pallas_call x1, Pallas kernels, local(): pl.pallas_call(functools.partial(_attend, n, g, scale), out_shape=jax.Sha...  9.65 us
    unnamed x1, local copies, waits for them, and re-layouts  2.65 us

profile of v1, /device:TPU:100, one launch (start us, length us, event | category | flops | bytes accessed | tf_op | source)
XLA Modules:
  0.0 98.8 jit_solution(6458877841352815598)
XLA Ops:
  0.0 52.3 %project.1 = (bf16[32,2,2,128,128]{4,3,2,1,0:T(8,128)(2,1)}, bf16[8,2,3,128,128]{4,3,2,1,0:T(8,128)(2,1)}, s32[32,2,128]{2,1,0:T(2,128)}) custom-call(bf16[256,3072]{1,0:T(8,128)(2,1)} %x_in.1, s32[1,2,128]{2,1,0:T(2,128)} %bitcast.1, bf16[3072,1024]{1,0:T(8,128)(2,1)} %wk.1, bf16[3072,1024]{1,0:T(8,128)(2,1)} %wv.1, bf16[3072,3072]{1,0:T(8,128)(2,1)} %wq.1), custom_call_target="tpu_custom_call" | custom-call | tf_op jit(solution)/shard_map/project/pallas_call | solution.py:628
  52.3 9.6 %attend.1.o_in = bf16[8,128,384]{2,1,0:T(8,128)(2,1)} custom-call(s32[32,2,128]{2,1,0:T(2,128)} %get-tuple-element.8.segs, bf16[32,2,2,128,128]{4,3,2,1,0:T(8,128)(2,1)} %get-tuple-element.9.kv, bf16[8,2,3,128,128]{4,3,2,1,0:T(8,128)(2,1)} %get-tuple-element.10.q_in), custom_call_target="tpu_custom_call" | custom-call | tf_op jit(solution)/shard_map/attend/pallas_call | solution.py:649
  61.9 34.2 %combine.1 = bf16[256,3072]{1,0:T(8,128)(2,1)} custom-call(s32[32,2,128]{2,1,0:T(2,128)} %get-tuple-element.8.segs, bf16[32,2,2,128,128]{4,3,2,1,0:T(8,128)(2,1)} %get-tuple-element.9.kv, bf16[8,2,3,128,128]{4,3,2,1,0:T(8,128)(2,1)} %get-tuple-element.10.q_in, bf16[8,128,384]{2,1,0:T(8,128)(2,1)} %attend.1.o_in, bf16[3072,3072]{1,0:T(8,128)(2,1)} %wo.1), custom_call_target="tpu_custom_call" | custom-call | tf_op jit(solution)/shard_map/combine/pallas_call | solution.py:660
  96.1 2.7 %copy.8 = bf16[256,3072]{1,0:T(8,128)(2,1)} copy(bf16[256,3072]{1,0:T(8,128)(2,1)} %combine.1) | data formatting | bytes 3145728

commit v2 on v1

--- a/solution.py
+++ b/solution.py
@@ -229,6 +229,11 @@
     for t in range(len(KV_ORDER)):
         send_kv(t)
     forward_own()
+
+    @pl.loop(1, n)
+    def _(i):
+        seg_copy(i).start()
+
     q_step(0, 0, nq)
     q_step(1, 0, nq)
     q_step(2, 0, nq)
@@ -264,10 +269,6 @@
         put(rq.at[hop], rq.at[hop], q_send.at[0], rq_recv.at[hop], me).wait_recv()
         q_hand(*hop).start()
     pass_on(passing[4:])
-
-    @pl.loop(1, n)
-    def _(i):
-        seg_copy(i).start()
 
     for t, dx, dy in passing:
         src = pt.dev(pt.col(dx), pt.row(-dy), 1 - pt.c)

time: 98.9 us -> 99.7 us (level)
    pallas_call x1, Pallas kernels: 9.65 us -> 14 us  [local(): pl.pallas_call(functools.partial(_attend, n, g, scale), out_shape=jax.Sha...]
    pallas_call x1, Pallas kernels: 34.2 us -> 31.9 us  [local(): pl.pallas_call(functools.partial(_combine, n, g, scale), out_shape=jax.Sh...]
    pallas_call x1, Pallas kernels: 52.3 us -> 51.1 us  [local(): pl.pallas_call(functools.partial(_project, n, g), out_shape=(jax.ShapeDty...]
where the time goes in v2:
time: 99.7 us
  Pallas kernels  97 us (97%)
  local copies, waits for them, and re-layouts  2.65 us (3%)
    pallas_call x1, Pallas kernels, local(): pl.pallas_call(functools.partial(_project, n, g), out_shape=(jax.ShapeDty...  51.1 us
    pallas_call x1, Pallas kernels, local(): pl.pallas_call(functools.partial(_combine, n, g, scale), out_shape=jax.Sh...  31.9 us
    pallas_call x1, Pallas kernels, local(): pl.pallas_call(functools.partial(_attend, n, g, scale), out_shape=jax.Sha...  14 us
    unnamed x1, local copies, waits for them, and re-layouts  2.65 us

profile of v2, /device:TPU:100, one launch (start us, length us, event | category | flops | bytes accessed | tf_op | source)
XLA Modules:
  0.0 99.7 jit_solution(8472731842985986413)
XLA Ops:
  0.0 51.1 %project.1 = (bf16[32,2,2,128,128]{4,3,2,1,0:T(8,128)(2,1)}, bf16[8,2,3,128,128]{4,3,2,1,0:T(8,128)(2,1)}, s32[32,2,128]{2,1,0:T(2,128)}) custom-call(bf16[256,3072]{1,0:T(8,128)(2,1)} %x_in.1, s32[1,2,128]{2,1,0:T(2,128)} %bitcast.1, bf16[3072,1024]{1,0:T(8,128)(2,1)} %wk.1, bf16[3072,1024]{1,0:T(8,128)(2,1)} %wv.1, bf16[3072,3072]{1,0:T(8,128)(2,1)} %wq.1), custom_call_target="tpu_custom_call" | custom-call | tf_op jit(solution)/shard_map/project/pallas_call | solution.py:629
  51.2 14.0 %attend.1.o_in = bf16[8,128,384]{2,1,0:T(8,128)(2,1)} custom-call(s32[32,2,128]{2,1,0:T(2,128)} %get-tuple-element.8.segs, bf16[32,2,2,128,128]{4,3,2,1,0:T(8,128)(2,1)} %get-tuple-element.9.kv, bf16[8,2,3,128,128]{4,3,2,1,0:T(8,128)(2,1)} %get-tuple-element.10.q_in), custom_call_target="tpu_custom_call" | custom-call | tf_op jit(solution)/shard_map/attend/pallas_call | solution.py:650
  65.1 31.9 %combine.1 = bf16[256,3072]{1,0:T(8,128)(2,1)} custom-call(s32[32,2,128]{2,1,0:T(2,128)} %get-tuple-element.8.segs, bf16[32,2,2,128,128]{4,3,2,1,0:T(8,128)(2,1)} %get-tuple-element.9.kv, bf16[8,2,3,128,128]{4,3,2,1,0:T(8,128)(2,1)} %get-tuple-element.10.q_in, bf16[8,128,384]{2,1,0:T(8,128)(2,1)} %attend.1.o_in, bf16[3072,3072]{1,0:T(8,128)(2,1)} %wo.1), custom_call_target="tpu_custom_call" | custom-call | tf_op jit(solution)/shard_map/combine/pallas_call | solution.py:661
  97.0 2.7 %copy.8 = bf16[256,3072]{1,0:T(8,128)(2,1)} copy(bf16[256,3072]{1,0:T(8,128)(2,1)} %combine.1) | data formatting | bytes 3145728
